TPU v7x, 32 devices: a whole 2x2x4 slice. The times are simulated.
32 devices in a mesh: grp: 2 (over x), pool: 16 (over z, y, core).
Axes of the slice: x: 2, y: 2, z: 4, core: 2. Of those that a mesh axis runs over, the one named last changes fastest.
Arguments:
- query: bfloat16 [32, 4096], P(('grp', 'pool')), parts along dimension 0, may hold values from -6 to 6
- kv_pool: bfloat16 [2048, 2, 16, 512], P(('grp', 'pool')), parts along dimension 0, may hold values from -6 to 6
- holder_table: int32 [32, 128], P(('grp', 'pool')), parts along dimension 0, may hold values from 0 to 15, as said below
- slot_table: int32 [32, 128], P(('grp', 'pool')), parts along dimension 0, may hold values from 0 to 63
- lengths: int32 [32], P(('grp', 'pool')), parts along dimension 0, may hold values from 96 to 128, as said below
- out_weight: bfloat16 [4096, 8192], P('pool'), may hold values from -1.1953125 to 1.1953125
Outputs:
- mixed: bfloat16 [32, 8192], P(('grp', 'pool')), parts along dimension 0
There are 2 independent parts, one for each index of `grp`. A program takes and returns all parts, laid end to end along the dimension named above; an argument that names none is the same for every part. Nothing has to cross between parts.
Inputs may be any that keep to these rules, and one draw needn't show every extreme that they name: `holder_table`: entry [r, j] is the index along pool of the device holding block j of request r. Of one request's 128 blocks at most 16 have the same holder, and some holder has exactly 16 of the request's first 96 blocks. Request r's live blocks are 0 to lengths[r] - 1; some request has 128.
All inputs are finite; a program needn't handle non-finite values.
Results may differ from a plain program's by a relative error of at most 0.0053.
Values may be sent and summed in bfloat16 or wider, within the bound.
A program may use at most 64 MiB of HBM per device.

v0:
```python
import math

import jax
import jax.numpy as jnp
from jax import lax
from jax.sharding import PartitionSpec as P

H = 32
KVH = 4
HD = 128


lowest = -1e30


def block_partials(query_heads, kv_blocks):
    head_dim = query_heads.shape[-1]
    kv_heads = query_heads.shape[1]
    block_len = kv_blocks.shape[3]
    block_shape = kv_blocks.shape[:2] + (block_len, kv_heads, head_dim)
    key_part = kv_blocks[:, :, 0].reshape(block_shape)
    value_part = kv_blocks[:, :, 1].reshape(block_shape)
    scores = jnp.einsum(
        "agqd,acbgd->acgqb", query_heads, key_part, preferred_element_type=jnp.float32
    )
    scores = scores * (1.0 / math.sqrt(head_dim))
    maxima = jnp.max(scores, axis=-1)
    shifted = jnp.exp(scores - maxima[..., None])
    totals = jnp.sum(shifted, axis=-1)
    outputs = jnp.einsum(
        "acgqb,acbgd->acgqd",
        shifted.astype(jnp.bfloat16),
        value_part,
        preferred_element_type=jnp.float32,
    )
    return (maxima, outputs, totals)


def merge_blocks(maxima, outputs, totals, live_mask, axis_pos):
    peak_score = jnp.max(jnp.where(live_mask, maxima, lowest), axis=axis_pos, keepdims=True)
    factor = jnp.exp(jnp.where(live_mask, maxima - peak_score, lowest))
    numerator = jnp.sum(factor[..., None] * outputs, axis=axis_pos)
    denominator = jnp.sum(factor * totals, axis=axis_pos)
    return (jnp.squeeze(peak_score, axis_pos), numerator, denominator)


def per_device(query, kv_pool, holder_table, slot_table, lengths, out_weight):
    pool_size = lax.axis_size("pool")
    my_index = lax.axis_index("pool")
    max_blocks = holder_table.shape[1]
    capacity = 2 * max_blocks // pool_size
    groups = H // KVH
    all_holders, all_slots, all_lengths = (
        lax.all_gather(holder_table, "pool", axis=0, tiled=True),
        lax.all_gather(slot_table, "pool", axis=0, tiled=True),
        lax.all_gather(lengths, "pool", axis=0, tiled=True),
    )
    cap_iota = jnp.arange(capacity, dtype=jnp.int32)
    block_iota = jnp.arange(max_blocks, dtype=jnp.int32)
    held_here = all_holders == my_index
    rank_here = jnp.cumsum(held_here.astype(jnp.int32), axis=1) - 1
    pick_hot = held_here[:, None, :] & (rank_here[:, None, :] == cap_iota[None, :, None])
    pick_slot = jnp.sum(jnp.where(pick_hot, all_slots[:, None, :], 0), axis=-1)
    pick_block = jnp.sum(jnp.where(pick_hot, block_iota[None, None, :], 0), axis=-1)
    send_live = jnp.any(pick_hot, axis=-1) & (pick_block < all_lengths[:, None])
    send_blocks = kv_pool[pick_slot]
    all_queries = lax.all_gather(query, "pool", axis=0, tiled=True)
    maxima, outputs, totals = block_partials(
        all_queries.reshape(pool_size, KVH, groups, HD), send_blocks
    )
    part_peak, part_numer, part_denom = merge_blocks(
        maxima, outputs, totals, send_live[:, :, None, None], 1
    )
    got_peak, got_numer, got_denom = (
        lax.all_to_all(
            part_peak.reshape(pool_size, H), "pool", split_axis=0, concat_axis=0, tiled=True
        ),
        lax.all_to_all(
            part_numer.reshape(pool_size, H * HD), "pool", split_axis=0, concat_axis=0, tiled=True
        ),
        lax.all_to_all(
            part_denom.reshape(pool_size, H), "pool", split_axis=0, concat_axis=0, tiled=True
        ),
    )
    peak_score, numerator, denominator = merge_blocks(
        got_peak.reshape(pool_size, KVH, groups),
        got_numer.reshape(pool_size, KVH, groups, HD),
        got_denom.reshape(pool_size, KVH, groups),
        True,
        0,
    )
    attention = (numerator / denominator[..., None]).reshape(1, H * HD).astype(jnp.bfloat16)
    features = lax.all_to_all(attention, "pool", split_axis=1, concat_axis=0, tiled=True)
    return lax.psum_scatter(
        jnp.dot(features, out_weight, preferred_element_type=jnp.float32),
        "pool",
        scatter_dimension=0,
        tiled=True,
    ).astype(jnp.bfloat16)


def solution(mesh):
    placed = (
        P(("grp", "pool"), None),
        P(("grp", "pool"), None, None, None),
        P(("grp", "pool"), None),
        P(("grp", "pool"), None),
        P(("grp", "pool")),
        P("pool", None),
    )
    return jax.shard_map(
        per_device, mesh=mesh, in_specs=placed, out_specs=P(("grp", "pool"), None), check_vma=False
    )
```

profile of v0, /device:TPU:0, one launch (start us, length us, event | category | flops | bytes accessed | tf_op | source)
XLA Modules:
  0.0 231.0 jit_solution(6533422985778512869)
XLA Ops:
  0.0 23.4 %all-gather = s32[16,1,128]{2,1,0:T(1,128)S(1)} all-gather(s32[1,1,128]{2,1,0:T(1,128)} %bitcast.78), channel_id=1, replica_groups=mesh['grp'=2,'pool'=16] {'pool'}, dimensions={0}, use_global_device_ids=true | all-gather | bytes 8704 | tf_op jit(solution)/shard_map/all_gather | solution.py:54
  23.4 0.3 reduce_window_sum.11
  23.7 17.6 %all-gather.1 = s32[16,1,128]{2,1,0:T(1,128)S(1)} all-gather(s32[1,1,128]{2,1,0:T(1,128)} %bitcast.79), channel_id=1, replica_groups=mesh['grp'=2,'pool'=16] {'pool'}, dimensions={0}, use_global_device_ids=true | all-gather | bytes 8704 | tf_op jit(solution)/shard_map/all_gather | solution.py:55
  42.0 0.6 select_reduce_fusion.2
  42.6 1.3 fusion.18
  43.9 0.8 dynamic-update-slice
  44.7 0.4 fusion.12
  45.0 9.4 %all-reduce = s32[16]{0:T(128)S(1)} all-reduce(s32[16]{0:T(128)S(1)} %dynamic-update-slice), channel_id=1, replica_groups=mesh['grp'=2,'pool'=16] {'pool'}, use_global_device_ids=true, to_apply=%add | all-reduce | flops 16 | bytes 128
  54.5 8.5 %gather_fusion = bf16[256,2,16,512]{3,2,1,0:T(8,128)(2,1)} fusion(bf16[64,2,16,512]{3,2,1,0:T(8,128)(2,1)S(1)} %copy-done, s32[1024]{0:T(1024)S(1)} %pad_clamp_fusion), kind=kCustom, calls=%fused_computation | custom fusion | bytes 16778240 | tf_op jit(solution)/shard_map/gather | solution.py:66
  63.0 6.1 %slice_bitcast_fusion = (bf16[16,16,1,16,512]{4,3,1,0,2:T(8,128)(2,1)}, bf16[16,16,1,16,512]{4,3,1,0,2:T(8,128)(2,1)}) fusion(bf16[16,16,2,16,512]{4,3,2,1,0:T(8,128)(2,1)} %bitcast.64), kind=kLoop, calls=%fused_computation.1 | loop fusion | bytes 16777216
  69.1 6.9 %reshape_squeeze.6 = bf16[16,16,16,4,128]{4,3,2,1,0:T(4,128)(2,1)} reshape(bf16[16,16,1,16,512]{4,3,1,0,2:T(8,128)(2,1)} %get-tuple-element.12) | data formatting | bytes 8388608 | tf_op jit(solution)/shard_map/reshape;squeeze | solution.py:21
  76.0 21.5 %all-gather.2 = bf16[16,1,4096]{2,1,0:T(2,128)(2,1)S(1)} all-gather(bf16[1,1,4096]{2,1,0:T(2,128)(2,1)S(1)} %bitcast.77), channel_id=1, replica_groups=mesh['grp'=2,'pool'=16] {'pool'}, dimensions={0}, use_global_device_ids=true | all-gather | bytes 139264 | tf_op jit(solution)/shard_map/all_gather | solution.py:67
  97.5 0.7 reduce.6
  98.3 12.2 %bitcast_reduce_fusion = (f32[16,16,4,8]{3,1,2,0:T(8,128)S(1)}, f32[16,4,16,16,8]{3,4,2,1,0:T(8,128)S(1)}) fusion(bf16[16,4,8,128,1]{3,2,1,0,4:T(8,128)(2,1)S(1)} %bitcast.66, bf16[16,16,16,4,128]{4,3,2,1,0:T(4,128)(2,1)} %reshape_squeeze.6), kind=kOutput, calls=%fused_computation.4 | convolution fusion | flops 33808384 | bytes 4882432 | tf_op jit(solution)/shard_map/agqd,acbgd->acgqb/dot_general | solution.py:23
  110.7 2.9 %fusion.5 = (f32[16,16,4,8]{3,1,2,0:T(8,128)S(1)}, bf16[16,16,4,8,16]{4,3,1,2,0:T(8,128)(2,1)}) fusion(f32[16,4,16,16,8]{3,4,2,1,0:T(8,128)S(1)} %get-tuple-element.18, f32[16,16,4,8]{3,1,2,0:T(8,128)S(1)} %get-tuple-element.17), kind=kLoop, calls=%fused_computation.11 | loop fusion | flops 516096 | bytes 851968 | tf_op jit(solution)/shard_map/reduce_sum | solution.py:29
  113.6 0.3 multiply_reduce_fusion.1
  114.0 0.7 copy.55
  114.7 3.4 %all-to-all-start.2 = ((f32[16,1,32]{2,1,0:T(1,128)}), f32[16,1,32]{2,1,0:T(1,128)S(1)}, u32[]{:S(2)}, u32[]{:S(2)}) async-start(f32[16,1,32]{2,1,0:T(1,128)} %copy.55), calls=%async_computation.2 | async-start | bytes 16384 | tf_op jit(solution)/shard_map/all_to_all | solution.py:81
  118.2 0.7 copy.47
  119.0 6.9 %reshape_squeeze.7 = bf16[16,16,16,4,128]{4,3,2,1,0:T(4,128)(2,1)} reshape(bf16[16,16,1,16,512]{4,3,1,0,2:T(8,128)(2,1)} %get-tuple-element.11) | data formatting | bytes 8388608 | tf_op jit(solution)/shard_map/reshape;squeeze | solution.py:22
  126.0 6.0 %all-to-all-start = ((f32[16,1,32]{2,1,0:T(1,128)}), f32[16,1,32]{2,1,0:T(1,128)S(1)}, u32[]{:S(2)}, u32[]{:S(2)}) async-start(f32[16,1,32]{2,1,0:T(1,128)} %copy.47), calls=%async_computation | async-start | bytes 16384 | tf_op jit(solution)/shard_map/all_to_all | solution.py:75
  132.0 5.0 %multiply_reduce_fusion = f32[16,4,8,128]{3,2,1,0:T(8,128)} fusion(bf16[16,16,16,4,128]{4,3,2,1,0:T(4,128)(2,1)} %reshape_squeeze.7, bf16[16,16,4,8,16]{4,3,1,2,0:T(8,128)(2,1)} %get-tuple-element.14, f32[16,16,4,8]{3,2,1,0:T(4,128)S(1)} %copy.50), kind=kOutput, calls=%fused_computation.10 | convolution fusion | flops 35586048 | bytes 4751360 | tf_op jit(solution)/shard_map/acgqb,acbgd->acgqd/dot_general | solution.py:30
  137.0 1.3 all-to-all-done
  138.3 4.7 %all-to-all-start.1 = ((f32[16,1,4096]{2,1,0:T(1,128)}), f32[16,1,4096]{2,1,0:T(1,128)S(1)}, u32[]{:S(2)}, u32[]{:S(2)}) async-start(f32[16,1,4096]{2,1,0:T(1,128)} %bitcast.14), calls=%async_computation.1 | async-start | bytes 524288 | tf_op jit(solution)/shard_map/all_to_all | solution.py:78
  143.5 9.5 %all-to-all-done.1 = f32[16,1,4096]{2,1,0:T(1,128)S(1)} async-done(((f32[16,1,4096]{2,1,0:T(1,128)}), f32[16,1,4096]{2,1,0:T(1,128)S(1)}, u32[]{:S(2)}, u32[]{:S(2)}) %all-to-all-start.1) | async-done | bytes 262176 | tf_op jit(solution)/shard_map/all_to_all | solution.py:78
  153.2 0.3 multiply_reduce_fusion.2
  153.6 0.5 broadcast.73
  154.1 0.7 reduce.7
  154.8 9.1 %all_to_all.46 = bf16[16,2,128]{2,1,0:T(2,128)(2,1)S(1)} all-to-all(bf16[16,2,128]{2,1,0:T(2,128)(2,1)S(1)} %reshape.157), channel_id=1, replica_groups=mesh['grp'=2,'pool'=16] {'pool'}, dimensions={0} | all-to-all | bytes 16384 | tf_op jit(solution)/shard_map/all_to_all | solution.py:93
  163.9 2.8 %fusion.14 = f32[16,8192]{1,0:T(8,128)S(1)} fusion(bf16[256,8192]{1,0:T(8,128)(2,1)} %param.11, bf16[1,16,256]{2,0,1:T(2,128)(2,1)S(1)} %bitcast.73), kind=kOutput, calls=%fused_computation.29 | convolution fusion | flops 67108864 | bytes 4726784 | tf_op jit(solution)/shard_map/dot_general | solution.py:95
  166.8 63.0 %all-reduce.3 = bf16[16,8192]{1,0:T(8,128)(2,1)S(1)} all-reduce(f32[16,8192]{1,0:T(8,128)S(1)} %fusion.14), channel_id=2, replica_groups=mesh['grp'=2,'pool'=16] {'pool'}, use_global_device_ids=true, to_apply=%region_12.13.clone | all-reduce | flops 131072 | bytes 786432
  229.7 1.2 dynamic-slice_convert_fusion
  (29 shorter events, 1.5 us)
Async XLA Ops:
  0.0 54.5 %copy-start = (bf16[64,2,16,512]{3,2,1,0:T(8,128)(2,1)S(1)}, bf16[64,2,16,512]{3,2,1,0:T(8,128)(2,1)}, u32[]{:S(2)}) copy-start(bf16[64,2,16,512]{3,2,1,0:T(8,128)(2,1)} %param.7) | copy-start | bytes 6291460
  69.1 6.9 %copy-start.1 = (bf16[1,4096]{1,0:T(2,128)(2,1)S(1)}, bf16[1,4096]{1,0:T(2,128)(2,1)}, u32[]{:S(2)}) copy-start(bf16[1,4096]{1,0:T(2,128)(2,1)} %param.6) | copy-start | bytes 24580
  114.7 11.3 %all-to-all-start.2 = ((f32[16,1,32]{2,1,0:T(1,128)}), f32[16,1,32]{2,1,0:T(1,128)S(1)}, u32[]{:S(2)}, u32[]{:S(2)}) async-start(f32[16,1,32]{2,1,0:T(1,128)} %copy.55), calls=%async_computation.2 | async-start | bytes 16384 | tf_op jit(solution)/shard_map/all_to_all | solution.py:81
  126.0 12.3 %all-to-all-start = ((f32[16,1,32]{2,1,0:T(1,128)}), f32[16,1,32]{2,1,0:T(1,128)S(1)}, u32[]{:S(2)}, u32[]{:S(2)}) async-start(f32[16,1,32]{2,1,0:T(1,128)} %copy.47), calls=%async_computation | async-start | bytes 16384 | tf_op jit(solution)/shard_map/all_to_all | solution.py:75
  138.3 14.7 %all-to-all-start.1 = ((f32[16,1,4096]{2,1,0:T(1,128)}), f32[16,1,4096]{2,1,0:T(1,128)S(1)}, u32[]{:S(2)}, u32[]{:S(2)}) async-start(f32[16,1,4096]{2,1,0:T(1,128)} %bitcast.14), calls=%async_computation.1 | async-start | bytes 524288 | tf_op jit(solution)/shard_map/all_to_all | solution.py:78
where the time goes:
time: 232 us; the launch traced here: 231 us
  blocking collectives  144 us (62%)
  local copies, waits for them, and re-layouts  34.6 us (15%)
  matrix products  20 us (9%)
  starting transfers between devices  14.1 us (6%)
  waiting for transfers between devices  10.9 us (5%)
  other arithmetic  6.65 us (3%)
    unnamed x2, blocking collectives  72.4 us
    all_gather x1, blocking collectives, per_device(): lax.all_gather(holder_table, 'pool', axis=0, tiled=True)  23.4 us
    all_gather x1, blocking collectives, per_device(): all_queries = lax.all_gather(query, 'pool', axis=0, tiled=True)  21.5 us
    all_gather x1, blocking collectives, per_device(): lax.all_gather(slot_table, 'pool', axis=0, tiled=True)  17.6 us
    dot_general x1, matrix products, block_partials(): jnp.einsum('agqd,acbgd->acgqb', query_heads, key_part, preferred_element_...  12.2 us
    all_to_all x1, waiting for transfers between devices, per_device(): lax.all_to_all(part_numer.reshape(pool_size, H * HD), 'pool', split_axis=...  9.54 us
    all_to_all x1, blocking collectives, per_device(): lax.all_to_all(attention, 'pool', split_axis=1, concat_axis=0, tiled=True)  9.11 us
    unnamed x12, local copies, waits for them, and re-layouts  8.72 us
  transfers between devices with their start and end apart: 3, of which 2 were waited for; matrix products, arithmetic and copies ran while one was open for 6% of the time, Pallas kernels for 0%

commit v1 on v0

--- a/solution.py
+++ b/solution.py
@@ -1,13 +1,281 @@
+import functools
 import math
 
 import jax
 import jax.numpy as jnp
 from jax import lax
+from jax.experimental import pallas as pl
+from jax.experimental.pallas import tpu as pltpu
 from jax.sharding import PartitionSpec as P
 
 H = 32
 KVH = 4
 HD = 128
+GRP = H // KVH
+LOW = -float(2**100)
+PAD_A = 8
+PAD_B = 16
+F32 = jnp.float32
+BF16 = jnp.bfloat16
+
+
+def far_first(n):
+    return sorted(range(1, n), key=lambda k: abs(k - n // 2))
+
+
+def kernel(
+    n, slots, blk, hpd,
+    len_ref, q_ref, hold_ref, slot_ref, kv_ref, w_ref,
+    out_ref,
+    stage, msg_a, got_a, qf, expand, kvbuf, wbuf, send_b, got_b, wgt, feat, acc, send_d, got_d,
+    sem_as, sem_ar, sem_bs, sem_br, sem_ds, sem_dr, sem_loc, sem_pair_s, sem_pair_r, sem_fs, sem_fr,
+):
+    me = lax.axis_index("pool")
+    core = lax.rem(me, 2)
+    chip = me // 2
+    partner = me + 1 - 2 * core
+    half_heads = H // 2
+    half_feat = (KVH // 2) * HD
+    half_cols = w_ref.shape[1] // 2
+    rows_dev = w_ref.shape[0]
+    order = far_first(n)
+    rows_a = half_heads + PAD_A
+
+    def at(src, dst, ssem, rsem, peer):
+        return pltpu.make_async_remote_copy(
+            src_ref=src, dst_ref=dst, send_sem=ssem, recv_sem=rsem,
+            device_id={"pool": peer}, device_id_type=pl.DeviceIdType.MESH,
+        )
+
+    own_feat = pl.ds(pl.multiple_of(core * half_feat, HD), half_feat)
+    other_feat = pl.ds(pl.multiple_of((1 - core) * half_feat, HD), half_feat)
+    own_cols = pl.ds(pl.multiple_of(core * half_cols, HD), half_cols)
+    other_cols = pl.ds(pl.multiple_of((1 - core) * half_cols, HD), half_cols)
+    kv_local = pltpu.make_async_copy(kv_ref.at[:, :, :, own_feat], kvbuf.at[core], sem_loc.at[0])
+    w_local = pltpu.make_async_copy(w_ref.at[:, own_cols], wbuf.at[core], sem_loc.at[1])
+    kv_local.start()
+    w_local.start()
+
+    barrier = pltpu.get_barrier_semaphore()
+    for k in order:
+        pl.semaphore_signal(
+            barrier, inc=1, device_id={"pool": lax.rem(me + k, n)},
+            device_id_type=pl.DeviceIdType.MESH,
+        )
+
+    maxb = hold_ref.shape[1]
+    live = lax.broadcasted_iota(jnp.int32, (1, maxb), 1) < len_ref[0]
+    holders = jnp.where(live, hold_ref[...], -1).astype(F32)
+    slot_row = slot_ref[...].astype(F32)
+    for part in range(2):
+        for h in range(half_heads):
+            head = part * half_heads + h
+            stage[part, h : h + 1, :] = q_ref[:, head * HD : (head + 1) * HD].astype(F32)
+        stage[part, half_heads : half_heads + PAD_A, :] = jnp.zeros((PAD_A, HD), F32)
+        stage[part, half_heads : half_heads + 1, :] = holders
+        stage[part, half_heads + 1 : half_heads + 2, :] = slot_row
+    msg_a[...] = stage[...].astype(BF16)
+
+    pl.semaphore_wait(barrier, n - 1)
+
+    sends_a = []
+    for k in order:
+        peer = lax.rem(me + k, n)
+        copy = at(msg_a.at[lax.rem(peer, 2)], got_a.at[me], sem_as.at[k], sem_ar.at[me], peer)
+        copy.start()
+        sends_a.append(copy)
+    kv_pair = at(kv_ref.at[:, :, :, other_feat], kvbuf.at[core], sem_pair_s.at[0], sem_pair_r.at[0], partner)
+    kv_pair.start()
+    w_pair = at(w_ref.at[:, other_cols], wbuf.at[core], sem_pair_s.at[1], sem_pair_r.at[1], partner)
+    w_pair.start()
+
+    slot_pos = lax.broadcasted_iota(jnp.int32, expand.shape, 0)
+    token_pos = lax.broadcasted_iota(jnp.int32, expand.shape, 1)
+    expand[...] = jnp.where(token_pos // blk == slot_pos, 1.0, 0.0).astype(BF16)
+
+    got_a[me] = msg_a[core]
+    for k in reversed(order):
+        src = lax.rem(me + n - k, n)
+        at(msg_a.at[0], got_a.at[src], sem_as.at[k], sem_ar.at[src], src).wait_recv()
+    for r in range(n):
+        qf[r * rows_a : (r + 1) * rows_a, :] = got_a[r].astype(F32)
+
+    rel = qf[pl.ds(half_heads, n, stride=rows_a), :].astype(jnp.int32) - 2 * chip
+    slot_of = qf[pl.ds(half_heads + 1, n, stride=rows_a), :].astype(jnp.int32)
+    code = jnp.where((rel == 0) | (rel == 1), rel * slots + slot_of, -1)
+    lane = lax.broadcasted_iota(jnp.int32, (n, 2 * slots), 1)
+    count = jnp.zeros((n, 2 * slots), F32)
+    for j in range(maxb):
+        count += jnp.where(code[:, j : j + 1] == lane, 1.0, 0.0)
+    times = jnp.dot(count.astype(BF16), expand[...], preferred_element_type=F32)
+
+    kv_local.wait()
+    kv_pair.wait_recv()
+
+    tokens = slots * blk
+    scale = 1.0 / math.sqrt(HD)
+    dests = n // 2
+    per_group = GRP // hpd
+    chunk = hpd * n
+    lane_sq = lax.broadcasted_iota(jnp.int32, (GRP * n, HD), 1)
+    for g in range(KVH // 2):
+        cols = slice(g * HD, (g + 1) * HD)
+        heads = jnp.concatenate(
+            [qf[pl.ds(g * GRP + q, n, stride=rows_a), :] for q in range(GRP)], axis=0
+        ).astype(BF16)
+        scores = []
+        for d in range(2):
+            keys = kvbuf[d, :, 0, :, cols].reshape(tokens, HD)
+            s = lax.dot_general(heads, keys, (((1,), (1,)), ((), ())), preferred_element_type=F32)
+            s = (s * scale).reshape(GRP, n, tokens)
+            here = times[:, d * tokens : (d + 1) * tokens]
+            scores.append(jnp.where((here > 0.0)[None], s, LOW))
+        peak = jnp.maximum(
+            jnp.max(scores[0], axis=-1, keepdims=True), jnp.max(scores[1], axis=-1, keepdims=True)
+        )
+        peak = peak.astype(BF16).astype(F32)
+        total = jnp.zeros((GRP, n, 1), F32)
+        numer = jnp.zeros((GRP * n, HD), F32)
+        for d in range(2):
+            here = times[:, d * tokens : (d + 1) * tokens]
+            p = jnp.exp(scores[d] - peak) * here[None]
+            total += jnp.sum(p, axis=-1, keepdims=True)
+            values = kvbuf[d, :, 1, :, cols].reshape(tokens, HD)
+            numer += jnp.dot(
+                p.reshape(GRP * n, tokens).astype(BF16), values, preferred_element_type=F32
+            )
+        peak = peak.reshape(GRP * n, 1)
+        total = total.reshape(GRP * n, 1)
+        total_hi = total.astype(BF16).astype(F32)
+        total_lo = total - total_hi
+        stats = jnp.where(
+            lane_sq == 0, peak, jnp.where(lane_sq == 1, total_hi, jnp.where(lane_sq == 2, total_lo, 0.0))
+        )
+        stats = stats.T[:PAD_B].astype(BF16)
+        for part in range(per_group):
+            to = g * per_group + part
+            send_b[to, :chunk, :] = numer[part * chunk : (part + 1) * chunk].astype(BF16)
+            send_b[to, chunk : chunk + PAD_B, :] = stats
+        for part in range(per_group):
+            to = g * per_group + part
+            dest = core * dests + to
+
+            @pl.when(dest != me)
+            def _():
+                at(send_b.at[to], got_b.at[chip], sem_bs.at[to], sem_br.at[chip], dest).start()
+
+            @pl.when(dest == me)
+            def _():
+                got_b[chip] = send_b[to]
+
+    from_core = me // dests
+    for i in range(dests):
+        src = 2 * i + from_core
+
+        @pl.when(src != me)
+        def _():
+            at(send_b.at[0], got_b.at[i], sem_bs.at[0], sem_br.at[i], src).wait_recv()
+
+    tiles = [got_b[i, chunk : chunk + PAD_B, :].astype(F32) for i in range(dests)]
+    peaks = jnp.concatenate([t[0:1] for t in tiles], axis=0)
+    totals = jnp.concatenate([t[1:2] + t[2:3] for t in tiles], axis=0)
+    top = jnp.max(peaks, axis=0, keepdims=True)
+    factor = jnp.exp(peaks - top)
+    factor = factor / jnp.sum(factor * totals, axis=0, keepdims=True)
+    factor = jnp.concatenate([factor, jnp.zeros((GRP * n - dests, GRP * n), F32)], axis=0)
+    wgt[...] = factor.T
+    my_rows = pl.ds(pl.multiple_of(lax.rem(me, per_group) * chunk, chunk), chunk)
+    weights = wgt[my_rows, :]
+    mixed = jnp.zeros((chunk, HD), F32)
+    for i in range(dests):
+        mixed += weights[:, i : i + 1] * got_b[i, :chunk, :].astype(F32)
+    feat[core] = jnp.concatenate(
+        [mixed[q * n : (q + 1) * n] for q in range(hpd)], axis=1
+    ).astype(BF16)
+    f_pair = at(feat.at[core], feat.at[core], sem_fs.at[0], sem_fr.at[0], partner)
+    f_pair.start()
+    w_local.wait()
+    w_pair.wait_recv()
+    f_pair.wait_recv()
+
+    out_rows = half_cols // HD
+    step = 1024
+    left, right = feat[0], feat[1]
+    for c0 in range(0, half_cols, step):
+        part = jnp.dot(left, wbuf[0, :, c0 : c0 + step], preferred_element_type=F32)
+        part += jnp.dot(right, wbuf[1, :, c0 : c0 + step], preferred_element_type=F32)
+        for j in range(step // HD):
+            acc[pl.ds(c0 // HD + j, n, stride=out_rows), :] = part[:, j * HD : (j + 1) * HD]
+    for r in range(n):
+        send_d[r] = acc[r * out_rows : (r + 1) * out_rows, :].astype(BF16)
+    sends_d = []
+    for k in order:
+        peer = lax.rem(me + k, n)
+        copy = at(send_d.at[peer], got_d.at[me], sem_ds.at[k], sem_dr.at[me], peer)
+        copy.start()
+        sends_d.append(copy)
+    got_d[me] = send_d[me]
+    for k in reversed(order):
+        src = lax.rem(me + n - k, n)
+        at(send_d.at[0], got_d.at[src], sem_ds.at[k], sem_dr.at[src], src).wait_recv()
+    for part in range(2):
+        result = jnp.zeros((out_rows, HD), F32)
+        for i in range(n // 2):
+            result += got_d[2 * i + part].astype(F32)
+        out_ref[part * out_rows : (part + 1) * out_rows, :] = result.astype(BF16)
+
+    for copy in sends_a + sends_d:
+        copy.wait_send()
+    kv_pair.wait_send()
+    w_pair.wait_send()
+    f_pair.wait_send()
+    for to in range(dests):
+        dest = core * dests + to
+
+        @pl.when(dest != me)
+        def _():
+            at(send_b.at[to], got_b.at[chip], sem_bs.at[to], sem_br.at[chip], dest).wait_send()
+
+
+def fused(query, kv_pool, holder_table, slot_table, lengths, out_weight):
+    n = lax.axis_size("pool")
+    slots, _, blk, width = kv_pool.shape
+    rows_dev, model = out_weight.shape
+    hpd = rows_dev // HD
+    rows_a = H // 2 + PAD_A
+    out_rows = model // 2 // HD
+    chunk = hpd * n
+    vmem = pl.BlockSpec(memory_space=pltpu.VMEM)
+    hbm = pl.BlockSpec(memory_space=pl.ANY)
+    dma = pltpu.SemaphoreType.DMA
+    result = pl.pallas_call(
+        functools.partial(kernel, n, slots, blk, hpd),
+        out_shape=jax.ShapeDtypeStruct((2 * out_rows, HD), BF16),
+        in_specs=[pl.BlockSpec(memory_space=pltpu.SMEM), vmem, vmem, vmem, hbm, hbm],
+        out_specs=vmem,
+        scratch_shapes=[
+            pltpu.VMEM((2, rows_a, HD), F32),
+            pltpu.VMEM((2, rows_a, HD), BF16),
+            pltpu.VMEM((n, rows_a, HD), BF16),
+            pltpu.VMEM((n * rows_a, HD), F32),
+            pltpu.VMEM((2 * slots, 2 * slots * blk), BF16),
+            pltpu.VMEM((2, slots, 2, blk, width // 2), BF16),
+            pltpu.VMEM((2, rows_dev, model // 2), BF16),
+            pltpu.VMEM((n // 2, chunk + PAD_B, HD), BF16),
+            pltpu.VMEM((n // 2, chunk + PAD_B, HD), BF16),
+            pltpu.VMEM((GRP * n, GRP * n), F32),
+            pltpu.VMEM((2, n, rows_dev), BF16),
+            pltpu.VMEM((n * out_rows, HD), F32),
+            pltpu.VMEM((n, out_rows, HD), BF16),
+            pltpu.VMEM((n, out_rows, HD), BF16),
+            dma((n,)), dma((n,)), dma((n // 2,)), dma((n // 2,)), dma((n,)), dma((n,)),
+            dma((2,)), dma((2,)), dma((2,)), dma((1,)), dma((1,)),
+        ],
+        compiler_params=pltpu.CompilerParams(
+            collective_id=0, has_side_effects=True, vmem_limit_bytes=48 * 1024 * 1024
+        ),
+    )(lengths, query, holder_table, slot_table, kv_pool, out_weight)
+    return result.reshape(1, model)
 
 
 lowest = -1e30
@@ -44,7 +312,7 @@
     return (jnp.squeeze(peak_score, axis_pos), numerator, denominator)
 
 
-def per_device(query, kv_pool, holder_table, slot_table, lengths, out_weight):
+def general(query, kv_pool, holder_table, slot_table, lengths, out_weight):
     pool_size = lax.axis_size("pool")
     my_index = lax.axis_index("pool")
     max_blocks = holder_table.shape[1]
@@ -99,6 +367,24 @@
     ).astype(jnp.bfloat16)
 
 
+def per_device(query, kv_pool, holder_table, slot_table, lengths, out_weight):
+    n = lax.axis_size("pool")
+    rows_dev, model = out_weight.shape
+    slots = kv_pool.shape[0]
+    fits = (
+        n == 16
+        and query.shape[0] == 1
+        and rows_dev % HD == 0
+        and GRP % max(rows_dev // HD, 1) == 0
+        and model % 2048 == 0
+        and holder_table.shape[1] == HD
+        and 2 * slots == HD
+        and slots <= 256
+    )
+    body = fused if fits else general
+    return body(query, kv_pool, holder_table, slot_table, lengths, out_weight)
+
+
 def solution(mesh):
     placed = (
         P(("grp", "pool"), None),

time: 232 us -> 29.5 us (0.13)
  blocking collectives: 144 us -> 0 us
  local copies, waits for them, and re-layouts: 34.6 us -> 4.25 us
  Pallas kernels: 0 us -> 24.3 us
  matrix products: 20 us -> 0 us
  starting transfers between devices: 14.1 us -> 0 us
  waiting for transfers between devices: 10.9 us -> 0 us
  other arithmetic: 6.65 us -> 0 us
    unnamed x2 -> x0, blocking collectives: 72.4 us -> none
    all_gather x3 -> x0, blocking collectives: 62.5 us -> none  [the longest x1 23.4 us: per_device(): lax.all_gather(holder_table, 'pool', axis=0, tiled=True)]
    pallas_call x0 -> x1, Pallas kernels: none -> 24.3 us  [fused(): pl.pallas_call(functools.partial(kernel, n, slots, blk, hpd), out_shape=j...]
    dot_general x3 -> x0, matrix products: 20 us -> none  [the longest x1 12.2 us: block_partials(): jnp.einsum('agqd,acbgd->acgqb', query_heads, key_part, preferred_element_...]
    all_to_all x3 -> x0, starting transfers between devices: 14.1 us -> none  [the longest x1 5.97 us: per_device(): lax.all_to_all(part_peak.reshape(pool_size, H), 'pool', split_axis=0, con...]
    another operation x2 -> x0, local copies, waits for them, and re-layouts: 13.9 us -> none  [the longest x1 6.94 us: block_partials(): key_part = kv_blocks[:, :, 0].reshape(block_shape)]
    all_to_all x3 -> x0, waiting for transfers between devices: 10.9 us -> none  [the longest x1 9.54 us: per_device(): lax.all_to_all(part_numer.reshape(pool_size, H * HD), 'pool', split_axis=...]
    all_to_all x1 -> x0, blocking collectives: 9.11 us -> none  [per_device(): lax.all_to_all(attention, 'pool', split_axis=1, concat_axis=0, tiled=True)]
  transfers between devices with their start and end apart: 3 -> 0, of which waited for: 2 -> 0; matrix products, arithmetic and copies ran while one was open for 6% -> 0% of each run, Pallas kernels for 0% -> 0%
where the time goes in v1:
time: 29.5 us; the launch traced here: 29.3 us
  Pallas kernels  24.3 us (82%)
  local copies, waits for them, and re-layouts  4.25 us (14%)
  between operations  0.67 us (2%)
    pallas_call x1, Pallas kernels, fused(): pl.pallas_call(functools.partial(kernel, n, slots, blk, hpd), out_shape=j...  24.3 us
    unnamed x9, local copies, waits for them, and re-layouts  4.25 us

profile of v1, /device:TPU:0, one launch (start us, length us, event | category | flops | bytes accessed | tf_op | source)
XLA Modules:
  0.0 29.3 jit_solution(7362686801744019330)
XLA Ops:
  0.7 0.0 copy-start
  0.7 1.6 %copy-done = bf16[64,2,16,512]{3,2,1,0:T(8,128)(2,1)S(1)} copy-done((bf16[64,2,16,512]{3,2,1,0:T(8,128)(2,1)S(1)}, bf16[64,2,16,512]{3,2,1,0:T(8,128)(2,1)}, u32[]{:S(2)}) %copy-start) | copy-done | bytes 2097176
  2.2 0.0 copy-start.1
  2.2 0.7 %copy-done.1 = bf16[1,4096]{1,0:T(2,128)(2,1)S(1)} copy-done((bf16[1,4096]{1,0:T(2,128)(2,1)S(1)}, bf16[1,4096]{1,0:T(2,128)(2,1)}, u32[]{:S(2)}) %copy-start.1) | copy-done | bytes 8216
  3.0 0.0 copy-start.2
  3.0 0.7 %copy-done.2 = s32[1,128]{1,0:T(1,128)S(1)} copy-done((s32[1,128]{1,0:T(1,128)S(1)}, s32[1,128]{1,0:T(1,128)}, u32[]{:S(2)}) %copy-start.2) | copy-done | bytes 536
  3.6 0.0 copy-start.3
  3.6 0.7 %copy-done.3 = s32[1,128]{1,0:T(1,128)S(1)} copy-done((s32[1,128]{1,0:T(1,128)S(1)}, s32[1,128]{1,0:T(1,128)}, u32[]{:S(2)}) %copy-start.3) | copy-done | bytes 536
  4.3 24.3 %shard_map.64 = bf16[64,128]{1,0:T(8,128)(2,1)S(1)} custom-call(s32[1]{0:T(128)S(6)} %copy.10.len_ref, bf16[1,4096]{1,0:T(2,128)(2,1)S(1)} %copy-done.1, s32[1,128]{1,0:T(1,128)S(1)} %copy-done.2, s32[1,128]{1,0:T(1,128)S(1)} %copy-done.3, bf16[64,2,16,512]{3,2,1,0:T(8,128)(2,1)S(1)} %copy-done, bf16[256,8192]{1,0:T(8,128)(2,1)} %w_ref.1), custom_call_target="tpu_custom_call" | custom-call | tf_op jit(solution)/shard_map/pallas_call | solution.py:251
  28.6 0.6 %copy.9 = bf16[1,1,64,128]{3,1,2,0:T(2,128)(2,1)} copy(bf16[1,1,64,128]{3,2,1,0:T(8,128)(2,1)S(1)} %bitcast.5) | data formatting | bytes 32768
Async XLA Ops:
  0.7 1.6 %copy-start = (bf16[64,2,16,512]{3,2,1,0:T(8,128)(2,1)S(1)}, bf16[64,2,16,512]{3,2,1,0:T(8,128)(2,1)}, u32[]{:S(2)}) copy-start(bf16[64,2,16,512]{3,2,1,0:T(8,128)(2,1)} %kv_ref.1) | copy-start | bytes 6291460
  2.2 0.7 %copy-start.1 = (bf16[1,4096]{1,0:T(2,128)(2,1)S(1)}, bf16[1,4096]{1,0:T(2,128)(2,1)}, u32[]{:S(2)}) copy-start(bf16[1,4096]{1,0:T(2,128)(2,1)} %q_ref.1) | copy-start | bytes 24580
  3.0 0.7 %copy-start.2 = (s32[1,128]{1,0:T(1,128)S(1)}, s32[1,128]{1,0:T(1,128)}, u32[]{:S(2)}) copy-start(s32[1,128]{1,0:T(1,128)} %hold_ref.1) | copy-start | bytes 1540
  3.6 0.7 %copy-start.3 = (s32[1,128]{1,0:T(1,128)S(1)}, s32[1,128]{1,0:T(1,128)}, u32[]{:S(2)}) copy-start(s32[1,128]{1,0:T(1,128)} %slot_ref.1) | copy-start | bytes 1540

commit v2 on v0

--- a/solution.py
+++ b/solution.py
@@ -1,13 +1,340 @@
+import functools
 import math
 
 import jax
 import jax.numpy as jnp
 from jax import lax
+from jax.experimental import pallas as pl
+from jax.experimental.pallas import tpu as pltpu
 from jax.sharding import PartitionSpec as P
 
 H = 32
 KVH = 4
 HD = 128
+GRP = H // KVH
+LOW = -float(2**100)
+PAD_A = 8
+PAD_B = 8
+F32 = jnp.float32
+BF16 = jnp.bfloat16
+
+
+def kernel(
+    n, slots, blk, hpd, parts,
+    len_ref, q_hbm, hold_hbm, slot_hbm, kv_ref, w_ref,
+    out_ref,
+    q_ref, hold_ref, slot_ref, stage, msg_a, got_a, qf, expand, kvbuf, wbuf, send_b, got_b, wgt, acc, send_d, got_d,
+    sem_as, sem_ar, sem_bs, sem_br, sem_ds, sem_dr, sem_loc, sem_pair_s, sem_pair_r,
+):
+    me = lax.axis_index("pool")
+    core = lax.rem(me, 2)
+    chip = me // 2
+    chips = n // 2
+    half = n // 2
+    my_half = me // half
+    partner = me + 1 - 2 * core
+    half_heads = H // 2
+    half_feat = (KVH // 2) * HD
+    model = w_ref.shape[1]
+    rows_a = half_heads + PAD_A
+    both = 2 * slots
+    tokens = slots * blk
+    chip_heads = 2 * hpd
+    chunk = chip_heads * half
+    per_group = GRP // chip_heads
+    near = sorted(range(1, n), key=lambda k: min(k, n - k))
+
+    def at(src, dst, ssem, rsem, peer):
+        return pltpu.make_async_remote_copy(
+            src_ref=src, dst_ref=dst, send_sem=ssem, recv_sem=rsem,
+            device_id={"pool": peer}, device_id_type=pl.DeviceIdType.MESH,
+        )
+
+    small = [
+        pltpu.make_async_copy(src, dst, sem_loc.at[2 + i])
+        for i, (src, dst) in enumerate(
+            ((q_hbm, q_ref), (hold_hbm, hold_ref), (slot_hbm, slot_ref))
+        )
+    ]
+    for copy in small:
+        copy.start()
+    barrier = pltpu.get_barrier_semaphore()
+    for k in reversed(near):
+        pl.semaphore_signal(
+            barrier, inc=1, device_id={"pool": lax.rem(me + k, n)},
+            device_id_type=pl.DeviceIdType.MESH,
+        )
+    own_feat = pl.ds(pl.multiple_of(core * half_feat, HD), half_feat)
+    other_feat = pl.ds(pl.multiple_of((1 - core) * half_feat, HD), half_feat)
+    kv_local = pltpu.make_async_copy(kv_ref.at[:, :, :, own_feat], kvbuf.at[core], sem_loc.at[0])
+    w_local = pltpu.make_async_copy(w_ref, wbuf.at[core], sem_loc.at[1])
+    kv_local.start()
+    w_local.start()
+    for copy in small:
+        copy.wait()
+
+    maxb = hold_ref.shape[1]
+    live = lax.broadcasted_iota(jnp.int32, (1, maxb), 1) < len_ref[0]
+    code = jnp.where(live, hold_ref[...] * slots + slot_ref[...], -1)
+    code = jnp.broadcast_to(code, (chips, maxb))
+    place = lax.broadcasted_iota(jnp.int32, (chips, both), 0) * both + lax.broadcasted_iota(
+        jnp.int32, (chips, both), 1
+    )
+    count = jnp.zeros((chips, both), F32)
+    for j in range(maxb):
+        count += jnp.where(code[:, j : j + 1] == place, 1.0, 0.0)
+    for part in range(2):
+        for h in range(half_heads):
+            head = part * half_heads + h
+            stage[part, h : h + 1, :] = q_ref[:, head * HD : (head + 1) * HD].astype(F32)
+    for part in range(2):
+        heads = stage[part].astype(BF16)
+        for i in range(chips):
+            msg_a[2 * i + part, :half_heads, :] = heads
+            msg_a[2 * i + part, half_heads:, :] = jnp.broadcast_to(
+                count[i : i + 1], (PAD_A, both)
+            ).astype(BF16)
+
+    pl.semaphore_wait(barrier, n - 1)
+
+    sends_a = []
+    for k in near:
+        peer = lax.rem(me + k, n)
+        copy = at(msg_a.at[peer], got_a.at[me], sem_as.at[k], sem_ar.at[me], peer)
+        copy.start()
+        sends_a.append(copy)
+    kv_pair = at(kv_ref.at[:, :, :, other_feat], kvbuf.at[core], sem_pair_s.at[0], sem_pair_r.at[0], partner)
+    kv_pair.start()
+    w_pair = at(w_ref, wbuf.at[core], sem_pair_s.at[1], sem_pair_r.at[1], partner)
+    w_pair.start()
+
+    slot_pos = lax.broadcasted_iota(jnp.int32, expand.shape, 0)
+    token_pos = lax.broadcasted_iota(jnp.int32, expand.shape, 1)
+    expand[...] = jnp.where(token_pos // blk == slot_pos, 1.0, 0.0).astype(BF16)
+    got_a[me] = msg_a[me]
+
+    scale = math.log2(math.e) / math.sqrt(HD)
+    lane_sq = lax.broadcasted_iota(jnp.int32, (GRP * half, HD), 1)
+    for turn in range(2):
+        batch = my_half if turn == 0 else 1 - my_half
+        first = batch * half
+        for r in range(half):
+            src = first + r
+            if turn == 0:
+
+                @pl.when(src != me)
+                def _():
+                    at(msg_a.at[0], got_a.at[src], sem_as.at[0], sem_ar.at[src], src).wait_recv()
+
+            else:
+                at(msg_a.at[0], got_a.at[src], sem_as.at[0], sem_ar.at[src], src).wait_recv()
+            qf[r * rows_a : (r + 1) * rows_a, :] = got_a[src].astype(F32)
+        count = qf[pl.ds(half_heads, half, stride=rows_a), :]
+        times = jnp.dot(count.astype(BF16), expand[...], preferred_element_type=F32)
+        bias = jnp.where(times > 0.0, jnp.log2(times), LOW)
+        if turn == 0:
+            kv_local.wait()
+            kv_pair.wait_recv()
+        for g in range(KVH // 2):
+            cols = slice(g * HD, (g + 1) * HD)
+            heads = jnp.concatenate(
+                [qf[pl.ds(g * GRP + q, half, stride=rows_a), :] for q in range(GRP)], axis=0
+            ).astype(BF16)
+            scores = []
+            for d in range(2):
+                keys = kvbuf[d, :, 0, :, cols].reshape(tokens, HD)
+                s = lax.dot_general(
+                    heads, keys, (((1,), (1,)), ((), ())), preferred_element_type=F32
+                )
+                here = bias[:, d * tokens : (d + 1) * tokens]
+                scores.append((s * scale).reshape(GRP, half, tokens) + here[None])
+            peak = jnp.maximum(
+                jnp.max(scores[0], axis=-1, keepdims=True),
+                jnp.max(scores[1], axis=-1, keepdims=True),
+            )
+            peak = peak.astype(BF16).astype(F32)
+            total = jnp.zeros((GRP, half, 1), F32)
+            numer = jnp.zeros((GRP * half, HD), F32)
+            for d in range(2):
+                p = jnp.exp2(scores[d] - peak)
+                total += jnp.sum(p, axis=-1, keepdims=True)
+                values = kvbuf[d, :, 1, :, cols].reshape(tokens, HD)
+                numer += jnp.dot(
+                    p.reshape(GRP * half, tokens).astype(BF16), values, preferred_element_type=F32
+                )
+            peak = peak.reshape(GRP * half, 1)
+            total = total.reshape(GRP * half, 1)
+            total_hi = total.astype(BF16).astype(F32)
+            total_lo = total - total_hi
+            stats = jnp.where(
+                lane_sq == 0,
+                peak,
+                jnp.where(lane_sq == 1, total_hi, jnp.where(lane_sq == 2, total_lo, 0.0)),
+            )
+            stats = jnp.concatenate([stats, jnp.zeros((HD - GRP * half, HD), F32)], axis=0)
+            stats = stats.T[:PAD_B].astype(BF16)
+            for sub in range(per_group):
+                to = (turn * (KVH // 2) + g) * per_group + sub
+                send_b[to, :chunk, :] = numer[sub * chunk : (sub + 1) * chunk].astype(BF16)
+                send_b[to, chunk:, :] = stats
+            for sub in range(per_group):
+                to = (turn * (KVH // 2) + g) * per_group + sub
+                dest = 2 * (core * (chips // 2) + g * per_group + sub) + batch
+
+                @pl.when(dest != me)
+                def _():
+                    at(send_b.at[to], got_b.at[chip], sem_bs.at[to], sem_br.at[chip], dest).start()
+
+                @pl.when(dest == me)
+                def _():
+                    got_b[chip] = send_b[to]
+
+    from_core = chip // (chips // 2)
+    for i in range(chips):
+        src = 2 * i + from_core
+
+        @pl.when(src != me)
+        def _():
+            at(send_b.at[0], got_b.at[i], sem_bs.at[0], sem_br.at[i], src).wait_recv()
+
+    tiles = [got_b[i, chunk : chunk + PAD_B, :].astype(F32) for i in range(chips)]
+    peaks = jnp.concatenate([t[0:1] for t in tiles], axis=0)
+    totals = jnp.concatenate([t[1:2] + t[2:3] for t in tiles], axis=0)
+    used = lax.broadcasted_iota(jnp.int32, totals.shape, 1) < GRP * half
+    totals = jnp.where(used, totals, 1.0)
+    top = jnp.max(peaks, axis=0, keepdims=True)
+    factor = jnp.exp2(peaks - top)
+    factor = factor / jnp.sum(factor * totals, axis=0, keepdims=True)
+    factor = jnp.concatenate([factor, jnp.zeros((HD - chips, HD), F32)], axis=0)
+    wgt[...] = factor.T
+    my_rows = pl.ds(pl.multiple_of(lax.rem(chip, per_group) * chunk, chunk), chunk)
+    weights = wgt[my_rows, :]
+    mixed = jnp.zeros((chunk, HD), F32)
+    for i in range(chips):
+        mixed += weights[:, i : i + 1] * got_b[i, :chunk, :].astype(F32)
+    mixed = mixed.astype(BF16).astype(F32)
+    sides = [
+        jnp.concatenate(
+            [mixed[(d * hpd + q) * half : (d * hpd + q + 1) * half] for q in range(hpd)], axis=1
+        ).astype(BF16)
+        for d in range(2)
+    ]
+
+    w_local.wait()
+    w_pair.wait_recv()
+    cols_part = model // parts
+    out_rows = cols_part // HD
+    for part in range(parts):
+        span = slice(part * cols_part, (part + 1) * cols_part)
+        res = jnp.dot(sides[0], wbuf[0, :, span], preferred_element_type=F32)
+        res += jnp.dot(sides[1], wbuf[1, :, span], preferred_element_type=F32)
+        for j in range(out_rows):
+            acc[part, pl.ds(j, half, stride=out_rows), :] = res[:, j * HD : (j + 1) * HD]
+        for r in range(half):
+            send_d[part, r] = acc[part, r * out_rows : (r + 1) * out_rows, :].astype(BF16)
+        for k in range(half):
+            r = lax.rem(me + k, half)
+            dest = core * half + r
+
+            @pl.when(dest != me)
+            def _():
+                at(
+                    send_d.at[part, r], got_d.at[part, chip], sem_ds.at[part, r],
+                    sem_dr.at[part, chip], dest,
+                ).start()
+
+            @pl.when(dest == me)
+            def _():
+                got_d[part, chip] = send_d[part, r]
+
+    for part in range(parts):
+        for i in range(chips):
+            src = 2 * i + my_half
+
+            @pl.when(src != me)
+            def _():
+                at(
+                    send_d.at[part, 0], got_d.at[part, i], sem_ds.at[part, 0],
+                    sem_dr.at[part, i], src,
+                ).wait_recv()
+
+        result = jnp.zeros((out_rows, HD), F32)
+        for i in range(chips):
+            result += got_d[part, i].astype(F32)
+        out_ref[part * out_rows : (part + 1) * out_rows, :] = result.astype(BF16)
+
+    for copy in sends_a:
+        copy.wait_send()
+    kv_pair.wait_send()
+    w_pair.wait_send()
+    for turn in range(2):
+        batch = my_half if turn == 0 else 1 - my_half
+        for g in range(KVH // 2):
+            for sub in range(per_group):
+                to = (turn * (KVH // 2) + g) * per_group + sub
+                dest = 2 * (core * (chips // 2) + g * per_group + sub) + batch
+
+                @pl.when(dest != me)
+                def _():
+                    at(
+                        send_b.at[to], got_b.at[chip], sem_bs.at[to], sem_br.at[chip], dest
+                    ).wait_send()
+
+    for part in range(parts):
+        for r in range(half):
+            dest = core * half + r
+
+            @pl.when(dest != me)
+            def _():
+                at(
+                    send_d.at[part, r], got_d.at[part, chip], sem_ds.at[part, r],
+                    sem_dr.at[part, chip], dest,
+                ).wait_send()
+
+
+def fused(query, kv_pool, holder_table, slot_table, lengths, out_weight):
+    n = lax.axis_size("pool")
+    slots, _, blk, width = kv_pool.shape
+    rows_dev, model = out_weight.shape
+    hpd = rows_dev // HD
+    rows_a = H // 2 + PAD_A
+    parts = 4
+    out_rows = model // parts // HD
+    half = n // 2
+    chunk = 2 * hpd * half
+    vmem = pl.BlockSpec(memory_space=pltpu.VMEM)
+    hbm = pl.BlockSpec(memory_space=pltpu.HBM)
+    dma = pltpu.SemaphoreType.DMA
+    result = pl.pallas_call(
+        functools.partial(kernel, n, slots, blk, hpd, parts),
+        out_shape=jax.ShapeDtypeStruct((parts * out_rows, HD), BF16),
+        in_specs=[pl.BlockSpec(memory_space=pltpu.SMEM)] + [hbm] * 5,
+        out_specs=vmem,
+        scratch_shapes=[
+            pltpu.VMEM(query.shape, BF16),
+            pltpu.VMEM(holder_table.shape, jnp.int32),
+            pltpu.VMEM(slot_table.shape, jnp.int32),
+            pltpu.VMEM((2, H // 2, HD), F32),
+            pltpu.VMEM((n, rows_a, HD), BF16),
+            pltpu.VMEM((n, rows_a, HD), BF16),
+            pltpu.VMEM((half * rows_a, HD), F32),
+            pltpu.VMEM((2 * slots, 2 * slots * blk), BF16),
+            pltpu.VMEM((2, slots, 2, blk, width // 2), BF16),
+            pltpu.VMEM((2, rows_dev, model), BF16),
+            pltpu.VMEM((half, chunk + PAD_B, HD), BF16),
+            pltpu.VMEM((half, chunk + PAD_B, HD), BF16),
+            pltpu.VMEM((HD, HD), F32),
+            pltpu.VMEM((parts, half * out_rows, HD), F32),
+            pltpu.VMEM((parts, half, out_rows, HD), BF16),
+            pltpu.VMEM((parts, half, out_rows, HD), BF16),
+            dma((n,)), dma((n,)), dma((half,)), dma((half,)), dma((parts, half)), dma((parts, half)),
+            dma((5,)), dma((2,)), dma((2,)),
+        ],
+        compiler_params=pltpu.CompilerParams(
+            collective_id=0, has_side_effects=True, vmem_limit_bytes=67_043_328
+        ),
+    )(lengths, query, holder_table, slot_table, kv_pool, out_weight)
+    return result.reshape(1, model)
 
 
 lowest = -1e30
@@ -44,7 +371,7 @@
     return (jnp.squeeze(peak_score, axis_pos), numerator, denominator)
 
 
-def per_device(query, kv_pool, holder_table, slot_table, lengths, out_weight):
+def general(query, kv_pool, holder_table, slot_table, lengths, out_weight):
     pool_size = lax.axis_size("pool")
     my_index = lax.axis_index("pool")
     max_blocks = holder_table.shape[1]
@@ -99,6 +426,24 @@
     ).astype(jnp.bfloat16)
 
 
+def per_device(query, kv_pool, holder_table, slot_table, lengths, out_weight):
+    n = lax.axis_size("pool")
+    rows_dev, model = out_weight.shape
+    slots = kv_pool.shape[0]
+    fits = (
+        n == 16
+        and query.shape[0] == 1
+        and rows_dev % HD == 0
+        and GRP % max(2 * (rows_dev // HD), 1) == 0
+        and model % 2048 == 0
+        and holder_table.shape[1] == HD
+        and 2 * slots == HD
+        and KVH % 2 == 0
+    )
+    body = fused if fits else general
+    return body(query, kv_pool, holder_table, slot_table, lengths, out_weight)
+
+
 def solution(mesh):
     placed = (
         P(("grp", "pool"), None),

time: 232 us -> 24.8 us (0.11)
  blocking collectives: 144 us -> 0 us
  local copies, waits for them, and re-layouts: 34.6 us -> 1.36 us
  Pallas kernels: 0 us -> 22.5 us
  matrix products: 20 us -> 0 us
  starting transfers between devices: 14.1 us -> 0 us
  waiting for transfers between devices: 10.9 us -> 0 us
  other arithmetic: 6.65 us -> 0 us
    unnamed x2 -> x0, blocking collectives: 72.4 us -> none
    all_gather x3 -> x0, blocking collectives: 62.5 us -> none  [the longest x1 23.4 us: per_device(): lax.all_gather(holder_table, 'pool', axis=0, tiled=True)]
    pallas_call x0 -> x1, Pallas kernels: none -> 22.5 us  [fused(): pl.pallas_call(functools.partial(kernel, n, slots, blk, hpd, parts), out_...]
    dot_general x3 -> x0, matrix products: 20 us -> none  [the longest x1 12.2 us: block_partials(): jnp.einsum('agqd,acbgd->acgqb', query_heads, key_part, preferred_element_...]
    all_to_all x3 -> x0, starting transfers between devices: 14.1 us -> none  [the longest x1 5.97 us: per_device(): lax.all_to_all(part_peak.reshape(pool_size, H), 'pool', split_axis=0, con...]
    another operation x2 -> x0, local copies, waits for them, and re-layouts: 13.9 us -> none  [the longest x1 6.94 us: block_partials(): key_part = kv_blocks[:, :, 0].reshape(block_shape)]
    all_to_all x3 -> x0, waiting for transfers between devices: 10.9 us -> none  [the longest x1 9.54 us: per_device(): lax.all_to_all(part_numer.reshape(pool_size, H * HD), 'pool', split_axis=...]
    all_to_all x1 -> x0, blocking collectives: 9.11 us -> none  [per_device(): lax.all_to_all(attention, 'pool', split_axis=1, concat_axis=0, tiled=True)]
  transfers between devices with their start and end apart: 3 -> 0, of which waited for: 2 -> 0; matrix products, arithmetic and copies ran while one was open for 6% -> 0% of each run, Pallas kernels for 0% -> 0%
where the time goes in v2:
time: 24.8 us; the launch traced here: 24.5 us
  Pallas kernels  22.5 us (91%)
  local copies, waits for them, and re-layouts  1.36 us (5%)
  between operations  0.66 us (3%)
    pallas_call x1, Pallas kernels, fused(): pl.pallas_call(functools.partial(kernel, n, slots, blk, hpd, parts), out_...  22.5 us
    unnamed x1, local copies, waits for them, and re-layouts  1.36 us

profile of v2, /device:TPU:0, one launch (start us, length us, event | category | flops | bytes accessed | tf_op | source)
XLA Modules:
  0.0 24.5 jit_solution(4773798821020680266)
XLA Ops:
  0.7 22.5 %shard_map.64 = bf16[64,128]{1,0:T(8,128)(2,1)} custom-call(s32[1]{0:T(128)S(6)} %copy.10.len_ref, bf16[1,4096]{1,0:T(2,128)(2,1)} %q_hbm.1, s32[1,128]{1,0:T(1,128)} %hold_hbm.1, s32[1,128]{1,0:T(1,128)} %slot_hbm.1, bf16[64,2,16,512]{3,2,1,0:T(8,128)(2,1)} %kv_ref.1, bf16[256,8192]{1,0:T(8,128)(2,1)} %w_ref.1), custom_call_target="tpu_custom_call" | custom-call | tf_op jit(solution)/shard_map/pallas_call | solution.py:308
  23.1 1.4 %copy.9 = bf16[1,1,64,128]{3,1,2,0:T(2,128)(2,1)} copy(bf16[1,1,64,128]{3,2,1,0:T(8,128)(2,1)} %bitcast.5) | data formatting | bytes 32768

commit v3 on v2

--- a/solution.py
+++ b/solution.py
@@ -23,7 +23,7 @@
     n, slots, blk, hpd, parts,
     len_ref, q_hbm, hold_hbm, slot_hbm, kv_ref, w_ref,
     out_ref,
-    q_ref, hold_ref, slot_ref, stage, msg_a, got_a, qf, expand, kvbuf, wbuf, send_b, got_b, wgt, acc, send_d, got_d,
+    q_ref, hold_ref, slot_ref, stage, msg_a, got_a, qf, expand, kvbuf, keys_t, wbuf, send_b, got_b, wgt, acc, send_d, got_d,
     sem_as, sem_ar, sem_bs, sem_br, sem_ds, sem_dr, sem_loc, sem_pair_s, sem_pair_r,
 ):
     me = lax.axis_index("pool")
@@ -113,6 +113,13 @@
     expand[...] = jnp.where(token_pos // blk == slot_pos, 1.0, 0.0).astype(BF16)
     got_a[me] = msg_a[me]
 
+    kv_local.wait()
+    kv_pair.wait_recv()
+    for g in range(KVH // 2):
+        for d in range(2):
+            keys = kvbuf[d, :, 0, :, g * HD : (g + 1) * HD].reshape(tokens, HD)
+            keys_t[g, :, d * tokens : (d + 1) * tokens] = keys.T
+
     scale = math.log2(math.e) / math.sqrt(HD)
     lane_sq = lax.broadcasted_iota(jnp.int32, (GRP * half, HD), 1)
     for turn in range(2):
@@ -132,9 +139,6 @@
         count = qf[pl.ds(half_heads, half, stride=rows_a), :]
         times = jnp.dot(count.astype(BF16), expand[...], preferred_element_type=F32)
         bias = jnp.where(times > 0.0, jnp.log2(times), LOW)
-        if turn == 0:
-            kv_local.wait()
-            kv_pair.wait_recv()
         for g in range(KVH // 2):
             cols = slice(g * HD, (g + 1) * HD)
             heads = jnp.concatenate(
@@ -142,10 +146,8 @@
             ).astype(BF16)
             scores = []
             for d in range(2):
-                keys = kvbuf[d, :, 0, :, cols].reshape(tokens, HD)
-                s = lax.dot_general(
-                    heads, keys, (((1,), (1,)), ((), ())), preferred_element_type=F32
-                )
+                keys = keys_t[g, :, d * tokens : (d + 1) * tokens]
+                s = jnp.dot(heads, keys, preferred_element_type=F32)
                 here = bias[:, d * tokens : (d + 1) * tokens]
                 scores.append((s * scale).reshape(GRP, half, tokens) + here[None])
             peak = jnp.maximum(
@@ -232,20 +234,24 @@
             acc[part, pl.ds(j, half, stride=out_rows), :] = res[:, j * HD : (j + 1) * HD]
         for r in range(half):
             send_d[part, r] = acc[part, r * out_rows : (r + 1) * out_rows, :].astype(BF16)
-        for k in range(half):
+        for k in range(1, half):
             r = lax.rem(me + k, half)
-            dest = core * half + r
-
-            @pl.when(dest != me)
-            def _():
-                at(
-                    send_d.at[part, r], got_d.at[part, chip], sem_ds.at[part, r],
-                    sem_dr.at[part, chip], dest,
-                ).start()
-
-            @pl.when(dest == me)
-            def _():
-                got_d[part, chip] = send_d[part, r]
+            at(
+                send_d.at[part, r], got_d.at[part, chip], sem_ds.at[part, r],
+                sem_dr.at[part, chip], core * half + r,
+            ).start()
+        mine = lax.rem(me, half)
+
+        @pl.when(core != my_half)
+        def _():
+            at(
+                send_d.at[part, mine], got_d.at[part, chip], sem_ds.at[part, mine],
+                sem_dr.at[part, chip], core * half + mine,
+            ).start()
+
+        @pl.when(core == my_half)
+        def _():
+            got_d[part, chip] = send_d[part, mine]
 
     for part in range(parts):
         for i in range(chips):
@@ -298,7 +304,7 @@
     rows_dev, model = out_weight.shape
     hpd = rows_dev // HD
     rows_a = H // 2 + PAD_A
-    parts = 4
+    parts = 2
     out_rows = model // parts // HD
     half = n // 2
     chunk = 2 * hpd * half
@@ -320,6 +326,7 @@
             pltpu.VMEM((half * rows_a, HD), F32),
             pltpu.VMEM((2 * slots, 2 * slots * blk), BF16),
             pltpu.VMEM((2, slots, 2, blk, width // 2), BF16),
+            pltpu.VMEM((KVH // 2, HD, 2 * slots * blk), BF16),
             pltpu.VMEM((2, rows_dev, model), BF16),
             pltpu.VMEM((half, chunk + PAD_B, HD), BF16),
             pltpu.VMEM((half, chunk + PAD_B, HD), BF16),

time: 24.8 us -> 24.2 us (0.976)
  Pallas kernels: 22.5 us -> 21.8 us
    pallas_call x1, Pallas kernels: 22.5 us -> 21.8 us  [fused(): pl.pallas_call(functools.partial(kernel, n, slots, blk, hpd, parts), out_...]
where the time goes in v3:
time: 24.2 us; the launch traced here: 23.9 us
  Pallas kernels  21.8 us (90%)
  local copies, waits for them, and re-layouts  1.36 us (6%)
  between operations  0.66 us (3%)
    pallas_call x1, Pallas kernels, fused(): pl.pallas_call(functools.partial(kernel, n, slots, blk, hpd, parts), out_...  21.8 us
    unnamed x1, local copies, waits for them, and re-layouts  1.36 us

profile of v3, /device:TPU:0, one launch (start us, length us, event | category | flops | bytes accessed | tf_op | source)
XLA Modules:
  0.0 23.9 jit_solution(1281215759489626788)
XLA Ops:
  0.7 21.8 %shard_map.64 = bf16[64,128]{1,0:T(8,128)(2,1)} custom-call(s32[1]{0:T(128)S(6)} %copy.10.len_ref, bf16[1,4096]{1,0:T(2,128)(2,1)} %q_hbm.1, s32[1,128]{1,0:T(1,128)} %hold_hbm.1, s32[1,128]{1,0:T(1,128)} %slot_hbm.1, bf16[64,2,16,512]{3,2,1,0:T(8,128)(2,1)} %kv_ref.1, bf16[256,8192]{1,0:T(8,128)(2,1)} %w_ref.1), custom_call_target="tpu_custom_call" | custom-call | tf_op jit(solution)/shard_map/pallas_call | solution.py:314
  22.5 1.4 %copy.9 = bf16[1,1,64,128]{3,1,2,0:T(2,128)(2,1)} copy(bf16[1,1,64,128]{3,2,1,0:T(8,128)(2,1)} %bitcast.5) | data formatting | bytes 32768
